TPU v7x, 512 devices: a whole 4x8x8 slice. The times are simulated.
512 devices in a mesh: ctx: 64 (over y_lo, z, x), head: 8 (over y_hi, core).
Axes of the slice: x: 4, y: 8 (y_hi: 4, y_lo: 2; y = y_hi * 2 + y_lo), z: 8, core: 2. Of those that a mesh axis runs over, the one named last changes fastest.
Arguments:
- patches: bfloat16 [8192, 1280], P('ctx'), may hold values from -6 to 6
- patch_count: int32 [64], P('ctx'), may hold values from 1 to 128, as said below
- token_patch: int32 [8192], P('ctx'), may hold values from -1 to 127, as said below
- window_ids: int32 [8192], P('ctx'), may hold values from 1 to 8192, as said below
- text_embed: bfloat16 [8192, 4096], P('ctx', 'head'), may hold values from -200 to 200
- vit_norm_gain: float32 [1280], replicated, may hold values from 0.25 to 1.75
- vit_qkv: bfloat16 [1280, 3840], P(None, 'head'), may hold values from -0.15625 to 0.15625
- vit_qkv_bias: float32 [3840], P('head'), may hold values from -16 to 16
- vit_proj: bfloat16 [1280, 1280], P('head'), may hold values from -0.15625 to 0.15625
- vit_proj_bias: float32 [1280], replicated, may hold values from -1 to 1
- merge_norm_gain: float32 [1280], replicated, may hold values from 0.25 to 1.75
- merger: bfloat16 [1280, 4096], P('ctx', 'head'), may hold values from -0.15625 to 0.15625
- merger_bias: float32 [4096], P('head'), may hold values from -1 to 1
- llm_norm_gain: float32 [4096], replicated, may hold values from 0.25 to 1.75
- w_qkv: bfloat16 [4096, 6144], P('ctx', 'head'), may hold values from -0.09375 to 0.09375
- qkv_bias: float32 [6144], P('head'), may hold values from -16 to 16
Outputs:
- context: bfloat16 [8192, 4096], P('ctx', 'head')
Inputs may be any that keep to these rules, and one draw needn't show every extreme that they name: `patch_count`: at most 128 live slots on one ctx index, reached by some index in every draw. `token_patch`: among the tokens of one ctx index, each live slot 0 to patch_count - 1 of that index appears exactly once; all other tokens hold -1. `window_ids`: ids never fall along the slots; a window lies within the slots of one ctx index and holds at most 64 consecutive slots; some window holds exactly 64.
All inputs are finite; a program needn't handle non-finite values.
Results may differ from a plain program's by a relative error of at most 0.012.
The roundings to bfloat16 on the way count: a program that leaves them out, or rounds other values in their place, can miss the bound.
Values may be sent and summed in bfloat16 or wider, within the bound.
A program may use at most 64 MiB of HBM per device.

v0:
```python
import math

import jax
import jax.numpy as jnp
from jax import lax
from jax.sharding import PartitionSpec as P

VHD = 80
HD = 128
QH = 4


EPSILON = 1e-06
THETA = 1000000.0
MASKED = -1e30


def in_order(tiles, dim):
    tiles = jnp.moveaxis(tiles, 0, dim)
    lengths = tiles.shape
    return tiles.reshape(*lengths[:dim], lengths[dim] * lengths[dim + 1], *lengths[dim + 2 :])


def gather_together(arrays, axis, dims):
    vector = jnp.concatenate([a.reshape(-1) for a in arrays])
    lines, at, gathered = (lax.all_gather(vector, axis), 0, [])
    for a, dim in zip(arrays, dims):
        tiles = lines[:, at : at + a.size].reshape(-1, *a.shape)
        gathered.append(in_order(tiles, dim))
        at += a.size
    return tuple(gathered)


def in_blocks(value, dim, size):
    lengths = value.shape
    tiles = value.reshape(*lengths[:dim], size, lengths[dim] // size, *lengths[dim + 1 :])
    return jnp.moveaxis(tiles, dim, 0)


def sent_and_summed(value, axis, dim):
    size = lax.axis_size(axis)
    tiles = lax.all_to_all(in_blocks(value, dim, size), axis, 0, 0, tiled=True)
    return jnp.sum(tiles, axis=0)


def copy_for_each(value, axis):
    size = lax.axis_size(axis)
    return lax.all_to_all(
        jnp.broadcast_to(value[None], (size, *value.shape)), axis, 0, 0, tiled=True
    )


def gathered_copies(value, axis, dim):
    tiles = copy_for_each(value, axis)
    return in_order(tiles, dim)


def side_by_side(arrays, axis, dim, along):
    ends, at = ([], 0)
    for a in arrays[:-1]:
        at += a.shape[along]
        ends.append(at)
    both = jnp.concatenate(arrays, axis=along)
    return tuple(jnp.split(lax.all_gather(both, axis, axis=dim, tiled=True), ends, axis=along))


def rms_norm(rows, gain):
    values = rows.astype(jnp.float32)
    return (
        values * lax.rsqrt(jnp.mean(values * values, axis=-1, keepdims=True) + EPSILON) * gain
    ).astype(jnp.bfloat16)


def rotate(values, positions):
    head_size = values.shape[-1]
    half = head_size // 2
    steps = jnp.arange(half, dtype=jnp.float32) * (2.0 / head_size)
    frequency = jnp.exp(-math.log(THETA) * steps)
    angle = positions.astype(jnp.float32)[:, None] * frequency[None, :]
    cosine = jnp.cos(angle)[:, None, None, :]
    sine = jnp.sin(angle)[:, None, None, :]
    first = values[..., :half]
    second = values[..., half:]
    return jnp.concatenate(
        [first * cosine - second * sine, second * cosine + first * sine], axis=-1
    )


def vision_heads(normed, weight, bias, windows, count, head_size):
    slot_count = normed.shape[0]
    mixed = jnp.dot(normed, weight, preferred_element_type=jnp.float32) + bias
    heads = mixed.shape[1] // (3 * head_size)
    mixed = mixed.astype(jnp.bfloat16).reshape(slot_count, heads, 3, head_size)
    scores = jnp.einsum(
        "rhd,shd->hrs", mixed[:, :, 0], mixed[:, :, 1], preferred_element_type=jnp.float32
    ) * (1.0 / math.sqrt(head_size))
    index = jnp.arange(slot_count, dtype=jnp.int32)
    allowed = (windows[:, None] == windows[None, :]) & (
        (index[None, :] < count) | (index[:, None] == index[None, :])
    )
    scores = jnp.where(allowed[None], scores, MASKED)
    top = jnp.max(scores, axis=-1, keepdims=True)
    weights = jnp.where(allowed[None], jnp.exp(scores - top), 0.0)
    total = jnp.sum(weights, axis=-1)
    result = jnp.einsum(
        "hrs,shd->rhd",
        weights.astype(jnp.bfloat16),
        mixed[:, :, 2],
        preferred_element_type=jnp.float32,
    )
    return (
        (result / jnp.transpose(total)[:, :, None])
        .astype(jnp.bfloat16)
        .reshape(slot_count, heads * head_size)
    )


def attend_block(state, query, query_pos, key, value, key_pos, scale):
    top, total, summed_values = state
    scores = jnp.einsum("gjrd,sgd->gjrs", query, key, preferred_element_type=jnp.float32) * scale
    allowed = key_pos[None, :] <= query_pos[:, None]
    scores = jnp.where(allowed, scores, MASKED)
    new_top = jnp.maximum(top, jnp.max(scores, axis=-1))
    weights = jnp.where(allowed, jnp.exp(scores - new_top[..., None]), 0.0)
    factor = jnp.exp(top - new_top)
    total = total * factor + jnp.sum(weights, axis=-1)
    summed_values = summed_values * factor[..., None] + jnp.einsum(
        "gjrs,sgd->gjrd", weights.astype(jnp.bfloat16), value, preferred_element_type=jnp.float32
    )
    return (new_top, total, summed_values)


def visit_block(state, query, query_pos, key, value, key_pos, scale):
    return lax.cond(
        jnp.min(key_pos) <= jnp.max(query_pos),
        lambda inner: attend_block(inner, query, query_pos, key, value, key_pos, scale),
        lambda inner: inner,
        state,
    )


def body(
    patches,
    patch_count,
    token_patch,
    window_ids,
    text_embed,
    vit_norm_gain,
    vit_qkv,
    vit_qkv_bias,
    vit_proj,
    vit_proj_bias,
    merge_norm_gain,
    merger,
    merger_bias,
    llm_norm_gain,
    w_qkv,
    qkv_bias,
):
    ctx_index = lax.axis_index("ctx")
    tok_rows = patches.shape[0]
    half = tok_rows // 2
    merger_full, weight_full = gather_together((merger, w_qkv), "ctx", (0, 0))
    normed = rms_norm(patches, vit_norm_gain)
    attended = vision_heads(normed, vit_qkv, vit_qkv_bias, window_ids, patch_count[0], VHD)
    partial_value = jnp.dot(attended, vit_proj, preferred_element_type=jnp.float32)
    summed = sent_and_summed(partial_value, "head", 0)
    share_rows = summed.shape[0]
    own_rows = lax.dynamic_slice_in_dim(patches, lax.axis_index("head") * share_rows, share_rows, 0)
    vit_out = own_rows.astype(jnp.float32) + summed + vit_proj_bias
    merged_share = rms_norm(vit_out, merge_norm_gain)
    merged_in = gathered_copies(merged_share, "head", 0)
    image_sum = jnp.dot(merged_in, merger_full, preferred_element_type=jnp.float32)
    image = (image_sum + merger_bias).astype(jnp.bfloat16)
    picked = jnp.take(image, jnp.maximum(token_patch, 0), axis=0)
    stitched = jnp.where(token_patch[:, None] >= 0, picked, text_embed)
    whole = lax.all_gather(stitched, "head", axis=1, tiled=True)
    values = whole.astype(jnp.float32)
    llm_in = (
        values
        * lax.rsqrt(jnp.mean(values * values, axis=-1, keepdims=True) + EPSILON)
        * llm_norm_gain
    ).astype(jnp.bfloat16)
    projected = jnp.dot(llm_in, weight_full, preferred_element_type=jnp.float32)
    projected = projected + qkv_bias
    groups = projected.shape[1] // ((QH + 2) * HD)
    projected = projected.reshape(tok_rows, groups, QH + 2, HD)
    positions = ctx_index * tok_rows + jnp.arange(tok_rows, dtype=jnp.int32)
    turned = rotate(projected[:, :, : QH + 1], positions).astype(jnp.bfloat16)
    queries = turned[:, :, :QH].reshape(tok_rows, groups * QH * HD)
    key_rows = turned[:, :, QH].reshape(tok_rows, groups * HD)
    value_rows = projected[:, :, QH + 1].astype(jnp.bfloat16).reshape(tok_rows, groups * HD)
    first_pos = ctx_index * tok_rows + jnp.arange(half, dtype=jnp.int32)
    second_pos = first_pos + half
    scale = 1.0 / math.sqrt(HD)
    query_heads = jnp.transpose(queries.reshape(tok_rows, groups, QH, HD), (1, 2, 0, 3))
    blocks = (query_heads[:, :, :half], query_heads[:, :, half:])
    block_pos = (first_pos, second_pos)

    def fresh():
        return (
            jnp.full((groups, QH, half), MASKED, jnp.float32),
            jnp.zeros((groups, QH, half), jnp.float32),
            jnp.zeros((groups, QH, half, HD), jnp.float32),
        )

    key_piece, value_piece = side_by_side((key_rows, value_rows), "ctx", 0, 1)
    piece_rows = key_piece.shape[0]
    block_rows = math.gcd(piece_rows, tok_rows)
    block_count = piece_rows // block_rows
    key_piece = key_piece.reshape(block_count, block_rows, groups, HD)
    value_piece = value_piece.reshape(block_count, block_rows, groups, HD)

    def visit(index, states):
        key_block = lax.dynamic_index_in_dim(key_piece, index, 0, keepdims=False)
        value_block = lax.dynamic_index_in_dim(value_piece, index, 0, keepdims=False)
        row_index = index * block_rows + jnp.arange(block_rows, dtype=jnp.int32)
        updated = []
        for which in range(2):
            updated.append(
                visit_block(
                    states[which],
                    blocks[which],
                    block_pos[which],
                    key_block,
                    value_block,
                    row_index,
                    scale,
                )
            )
        return tuple(updated)

    carry = lax.fori_loop(0, block_count, visit, (fresh(), fresh()))
    outputs = []
    for state in carry:
        top, total, summed_values = state
        result = (summed_values / total[..., None]).astype(jnp.bfloat16)
        outputs.append(jnp.transpose(result, (2, 0, 1, 3)).reshape(half, groups * QH * HD))
    returned = outputs[1]
    return jnp.concatenate([outputs[0], returned], axis=0)


def solution(mesh):
    return jax.shard_map(
        body,
        mesh=mesh,
        in_specs=(
            P("ctx", None),
            P("ctx"),
            P("ctx"),
            P("ctx"),
            P("ctx", "head"),
            P(),
            P(None, "head"),
            P("head"),
            P("head", None),
            P(),
            P(),
            P("ctx", "head"),
            P("head"),
            P(),
            P("ctx", "head"),
            P("head"),
        ),
        out_specs=P("ctx", "head"),
        check_vma=False,
    )
```

profile of v0, /device:TPU:494, one launch (start us, length us, event | category | flops | bytes accessed | tf_op | source)
XLA Modules:
  0.0 1001.0 jit_solution(16095911677490909299)
XLA Ops:
  6.5 1.1 reshape.294
  9.8 1.1 fusion.46
  11.8 1.6 fusion.37
  14.3 1.1 fusion.49
  15.4 7.2 all-to-all-start
  22.6 19.3 %all-to-all-done = f32[8,16,1280]{2,1,0:T(8,128)S(1)} async-done(((f32[8,16,1280]{2,1,0:T(8,128)}), f32[8,16,1280]{2,1,0:T(8,128)S(1)}, u32[]{:S(2)}, u32[]{:S(2)}) %all-to-all-start) | async-done | bytes 655392 | tf_op jit(solution)/shard_map/all_to_all | solution.py:42
  41.9 0.9 multiply_reduce_fusion
  42.9 0.9 multiply_convert_fusion
  44.5 9.2 all-to-all-start.1
  53.7 270.0 %all-gather.9.cloned.1.call-done = bf16[3801088]{0:T(1024)(128)(2,1)} async-done(((bf16[59392]{0:T(1024)(128)(2,1)}), bf16[3801088]{0:T(1024)(128)(2,1)}) %all-gather.9.cloned.1.call-update) | async-done | bytes 7602192 | tf_op jit(solution)/shard_map/all_gather | solution.py:26
  323.8 9.8 reshape.308
  333.6 1.3 slice-done
  334.9 2.9 reshape_reshape.6
  337.8 1.7 fusion.36
  341.4 5.8 slice.58
  347.3 9.0 reshape_reshape.7
  356.3 15.8 %all-gather.5.cloned.1.call-done = bf16[128,4096]{1,0:T(8,128)(2,1)} async-done(((bf16[128,512]{1,0:T(8,128)(2,1)}), bf16[128,4096]{1,0:T(8,128)(2,1)}) %all-gather.5.cloned.1.call-update) | async-done | bytes 1048592 | tf_op jit(solution)/shard_map/all_gather | solution.py:177
  372.1 1.5 fusion.32
  373.6 4.2 convolution_add_fusion
  379.7 243.8 %all-gather.7.cloned.1.call-done = bf16[8192,256]{0,1:T(8,128)(2,1)} async-done(((bf16[128,256]{0,1:T(8,128)(2,1)}), bf16[8192,256]{0,1:T(8,128)(2,1)}) %all-gather.7.cloned.1.call-update) | async-done | bytes 4194320 | tf_op jit(solution)/shard_map/all_gather | solution.py:64
  623.4 3.9 fusion.68
  627.3 4.1 copy.52
  631.4 2.5 copy.53
  633.9 359.5 %while.26 = (s32[]{:T(128)}, f32[1,4,64]{2,1,0:T(4,128)S(1)}, f32[1,4,64]{2,1,0:T(4,128)S(1)}, f32[1,4,64,128]{3,2,1,0:T(8,128)S(1)}, f32[1,4,64]{2,1,0:T(4,128)...) while((s32[]{:T(128)}, f32[1,4,64]{2,1,0:T(4,128)S(1)}, ...), condition=%wide.region_18.19_spmd.clone.clone, body=%wide.region_8.18_spmd.clone.clone.sunk | while | flops 34293636 | bytes 1805501 | solution.py:233
  636.6 0.8 conditional.9
  642.3 0.8 conditional.9
  647.9 0.8 conditional.9
  653.5 0.8 conditional.9
  659.1 0.8 conditional.9
  698.4 0.8 conditional.9
  704.0 0.8 conditional.9
  709.7 0.8 conditional.9
  749.0 0.8 conditional.9
  754.6 0.8 conditional.9
  760.2 0.8 conditional.9
  765.8 0.8 conditional.9
  805.2 0.8 conditional.9
  810.8 0.8 conditional.9
  816.4 0.8 conditional.9
  850.1 0.9 conditional.9
  855.7 0.8 conditional.9
  861.3 0.8 conditional.9
  867.0 0.8 conditional.9
  911.9 0.8 conditional.9
  917.5 0.8 conditional.9
  956.8 0.8 conditional.9
  962.4 0.8 conditional.9
  968.1 0.8 conditional.9
  (1326 shorter events, 289.8 us)
Async XLA Ops:
  6.5 5.2 copy-start
  6.5 7.7 copy-start.1
  6.5 317.2 %all-gather.9.cloned.1.call-start = ((), (), s32[]{:S(2)}) async-start(), calls=%async_computation.4 | async-start | bytes 7720960 | tf_op jit(solution)/shard_map/all_gather | solution.py:26
  13.6 28.3 %copy-start.3 = (f32[1280]{0:T(1024)S(1)}, f32[1280]{0:T(1024)}, u32[]{:S(2)}) copy-start(f32[1280]{0:T(1024)} %param.31) | copy-start | bytes 15364
  13.8 29.0 %copy-start.5 = (f32[1280]{0:T(1024)S(1)}, f32[1280]{0:T(1024)}, u32[]{:S(2)}) copy-start(f32[1280]{0:T(1024)} %param.32) | copy-start | bytes 15364
  14.3 39.4 %copy-start.8 = (s32[128]{0:T(128)S(1)}, s32[128]{0:T(128)}, u32[]{:S(2)}) copy-start(s32[128]{0:T(128)} %param.24) | copy-start | bytes 1540
  15.4 26.5 %all-to-all-start = ((f32[8,16,1280]{2,1,0:T(8,128)}), f32[8,16,1280]{2,1,0:T(8,128)S(1)}, u32[]{:S(2)}, u32[]{:S(2)}) async-start(f32[8,16,1280]{2,1,0:T(8,128)} %fusion.49), calls=%async_computation | async-start | bytes 1310720 | tf_op jit(solution)/shard_map/all_to_all | solution.py:42
  44.5 293.3 %all-to-all-start.1 = ((bf16[8,16,1280]{2,1,0:T(8,128)(2,1)}), bf16[8,16,1280]{2,1,0:T(8,128)(2,1)S(1)}, u32[]{:S(2)}, u32[]{:S(2)}) async-start(bf16[8,16,1280]{2,1,0:T(8,128)(2,1)} %broadcast_in_dim.105), calls=%async_computation.1 | async-start | bytes 655360 | tf_op jit(solution)/shard_map/all_to_all | solution.py:48
  53.7 318.4 %all-gather.5.cloned.1.call-start = ((), (), s32[]{:S(2)}) async-start(), calls=%async_computation.2 | async-start | bytes 1179648 | tf_op jit(solution)/shard_map/all_gather | solution.py:177
  333.6 1.3 slice-start
  333.6 4.2 copy-start.7
  337.8 2.6 copy-start.2
  341.1 282.3 %all-gather.7.cloned.1.call-start = ((), (), s32[]{:S(2)}) async-start(), calls=%async_computation.3 | async-start | bytes 4259840 | tf_op jit(solution)/shard_map/all_gather | solution.py:64
  347.2 26.3 %copy-start.4 = (f32[4096]{0:T(1024)S(1)}, f32[4096]{0:T(1024)}, u32[]{:S(2)}) copy-start(f32[4096]{0:T(1024)} %param.35) | copy-start | bytes 49156
  347.2 26.3 %copy-start.6 = (f32[768]{0:T(1024)S(1)}, f32[768]{0:T(1024)}, u32[]{:S(2)}) copy-start(f32[768]{0:T(1024)} %param.37) | copy-start | bytes 9220
Sparse Core Ops, SparseCore 0:
  9.4 314.3 all-gather.8
  341.3 30.7 all-gather.4
  378.8 244.5 all-gather.6
where the time goes:
time: 1010 us; the launch traced here: 1000 us
  waiting for transfers between devices  549 us (54%)
  loops' own time  166 us (16%)
  local copies, waits for them, and re-layouts  94.3 us (9%)
  other arithmetic  86.8 us (9%)
  matrix products  74.5 us (7%)
  starting transfers between devices  16.4 us (2%)
  between operations  14.1 us (1%)
    all_gather x1, waiting for transfers between devices, gather_together(): lines, at, gathered = (lax.all_gather(vector, axis), 0, [])  270 us
    all_gather x1, waiting for transfers between devices, side_by_side(): lax.all_gather(both, axis, axis=dim, tiled=True)  244 us
    another operation x1, loops' own time, body(): carry = lax.fori_loop(0, block_count, visit, (fresh(), fresh()))  161 us
    squeeze x64, local copies, waits for them, and re-layouts, visit(): lax.dynamic_index_in_dim(value_piece, index, 0, keepdims=False)  50.3 us
    add x64, other arithmetic, visit(): row_index = index * block_rows + jnp.arange(block_rows, dtype=jnp.int32)  40.4 us
    dot_general x128, matrix products, attend_block(): jnp.einsum('gjrd,sgd->gjrs', query, key, preferred_element_type=jnp.float32)  35.3 us
    dot_general x128, matrix products, attend_block(): jnp.einsum('gjrs,sgd->gjrd', weights.astype(jnp.bfloat16), value, preferr...  30 us
    reduce_sum x128, other arithmetic, attend_block(): total = total * factor + jnp.sum(weights, axis=-1)  24.1 us
  transfers between devices with their start and end apart: 5, of which 4 were waited for; matrix products, arithmetic and copies ran while one was open for 4% of the time, Pallas kernels for 0%

commit v1 on v0

v1 whole, which is shorter than its diff:
```python
import functools
import math

import jax
import jax.numpy as jnp
from jax import lax
from jax.experimental import pallas as pl
from jax.experimental.pallas import tpu as pltpu
from jax.sharding import PartitionSpec as P

VHD = 80
HD = 128
QH = 4
EPSILON = 1e-06
THETA = 1000000.0
MASKED = -1e30

PAIR, DEEP, WIDE = 2, 8, 4
ROWS, CORES = 4, 2
F32 = jnp.float32
BF16 = jnp.bfloat16


def ring_steps(n):
    return n // 2, (n - 1) // 2


def iota(shape, dim):
    return lax.broadcasted_iota(jnp.int32, shape, dim)


class Place:
    def __init__(self):
        ctx = lax.axis_index("ctx")
        head = lax.axis_index("head")
        self.ctx, self.head = ctx, head
        self.pair = ctx // (DEEP * WIDE)
        self.deep = (ctx // WIDE) % DEEP
        self.wide = ctx % WIDE
        self.row = head // CORES
        self.core = head % CORES
        self.sign = 1 - 2 * self.core

    def at_ctx(self, pair, deep, wide):
        return ((pair * DEEP + deep) * WIDE + wide, self.head)

    def at_head(self, row, core):
        return (self.ctx, row * CORES + core)

    def other_pair(self):
        return self.at_ctx(1 - self.pair, self.deep, self.wide)

    def deep_at(self, step):
        return (self.deep + step + 2 * DEEP) % DEEP

    def wide_at(self, step):
        return (self.wide + step + 2 * WIDE) % WIDE

    def neighbours(self):
        found = [self.other_pair()]
        found += [self.at_ctx(self.pair, self.deep_at(s), self.wide) for s in ((1, -1) if DEEP > 2 else (1,))]
        found += [self.at_ctx(self.pair, self.deep, self.wide_at(s)) for s in ((1, -1) if WIDE > 2 else (1,))]
        found += [self.at_head((self.row + k) % ROWS, self.core) for k in range(1, ROWS)]
        found.append(self.at_head(self.row, 1 - self.core))
        return found


class Copies:
    def __init__(self, send_sems, recv_sems):
        self.send_sems, self.recv_sems = send_sems, recv_sems
        self.used = 0
        self.sent = []

    def take(self):
        self.used += 1
        return self.used - 1

    def send(self, ref, slot, device):
        copy = pltpu.make_async_remote_copy(
            src_ref=ref,
            dst_ref=ref,
            send_sem=self.send_sems.at[slot],
            recv_sem=self.recv_sems.at[slot],
            device_id=device,
            device_id_type=pl.DeviceIdType.MESH,
        )
        copy.start()
        self.sent.append(copy)

    def wait(self, ref, slot, device):
        pltpu.make_async_remote_copy(
            src_ref=ref,
            dst_ref=ref,
            send_sem=self.send_sems.at[slot],
            recv_sem=self.recv_sems.at[slot],
            device_id=device,
            device_id_type=pl.DeviceIdType.MESH,
        ).wait_recv()

    def drain(self):
        for copy in self.sent:
            copy.wait_send()


class Chain:
    def __init__(self, copies, place, bundle, along_deep):
        self.copies, self.place, self.bundle = copies, place, bundle
        self.n = DEEP if along_deep else WIDE
        self.along_deep = along_deep
        self.steps = ring_steps(self.n)
        self.slots = [
            [[copies.take() for _ in range(PAIR)] for _ in range(count)] for count in self.steps
        ]

    def index(self, step):
        return self.place.deep_at(step) if self.along_deep else self.place.wide_at(step)

    def device(self, step):
        p = self.place
        if self.along_deep:
            return p.at_ctx(p.pair, p.deep_at(step), p.wide)
        return p.at_ctx(p.pair, p.deep, p.wide_at(step))

    def send(self, way, k, j):
        if k >= self.steps[way]:
            return
        sign = self.place.sign * (1 if way == 0 else -1)
        pair = self.place.pair if j == 0 else 1 - self.place.pair
        self.copies.send(self.bundle(pair, self.index(-sign * k)), self.slots[way][k][j], self.device(sign))

    def start(self, j):
        for way in range(2):
            self.send(way, 0, j)

    def tick(self, k):
        for j in range(PAIR):
            for way in range(2):
                if k < self.steps[way]:
                    sign = self.place.sign * (1 if way == 0 else -1)
                    pair = self.place.pair if j == 0 else 1 - self.place.pair
                    self.copies.wait(
                        self.bundle(pair, self.index(-sign * (k + 1))), self.slots[way][k][j], self.device(sign)
                    )
                    self.send(way, k + 1, j)


class CtxGather:
    def __init__(self, copies, place, buf, first, second):
        self.copies, self.place, self.buf = copies, place, buf
        p = place
        self.swap = copies.take()
        self.first_wide = Chain(copies, p, lambda j, i: buf.at[(j, p.deep, i) + first], False)
        self.first_deep = Chain(copies, p, lambda j, i: buf.at[(j, i, slice(None)) + first], True)
        self.second_deep = Chain(copies, p, lambda j, i: buf.at[(j, i, p.wide) + second], True)
        self.second_wide = Chain(copies, p, lambda j, i: buf.at[(j, slice(None), i) + second], False)
        self.ticks = 0
        w, d = WIDE // 2, DEEP // 2
        self.last = max(w + d, d + w)

    def start(self):
        p = self.place
        self.copies.send(self.buf.at[p.pair, p.deep, p.wide], self.swap, p.other_pair())
        self.first_wide.start(0)
        self.second_deep.start(0)

    def swapped(self):
        p = self.place
        self.copies.wait(self.buf.at[1 - p.pair, p.deep, p.wide], self.swap, p.other_pair())
        self.first_wide.start(1)
        self.second_deep.start(1)

    def tick(self):
        t = self.ticks
        w, d = WIDE // 2, DEEP // 2
        if t < w:
            self.first_wide.tick(t)
            if t == w - 1:
                self.first_deep.start(0)
                self.first_deep.start(1)
        elif t < w + d:
            self.first_deep.tick(t - w)
        if t < d:
            self.second_deep.tick(t)
            if t == d - 1:
                self.second_wide.start(0)
                self.second_wide.start(1)
        elif t < w + d:
            self.second_wide.tick(t - d)
        self.ticks += 1

    def done(self):
        return self.ticks >= WIDE // 2 + DEEP // 2


class HeadGather:
    def __init__(self, copies, place, buf):
        self.copies, self.place, self.buf = copies, place, buf
        self.own = [copies.take() for _ in range(ROWS)]
        self.passed = [copies.take() for _ in range(1, ROWS)]

    def slot(self, back, core):
        return ((self.place.row - back + ROWS) % ROWS) * CORES + core

    def start(self):
        p = self.place
        mine = self.buf.at[p.head]
        for k in range(1, ROWS):
            self.copies.send(mine, self.own[k], p.at_head((p.row + k) % ROWS, p.core))
        self.copies.send(mine, self.own[0], p.at_head(p.row, 1 - p.core))

    def order(self):
        return [k for k in range(1, ROWS) if k != 2] + ([2] if ROWS > 2 else [])

    def pass_on(self):
        p = self.place
        for k in self.order():
            ref = self.buf.at[self.slot(k, p.core)]
            self.copies.wait(ref, self.own[k], p.at_head(p.row, 1 - p.core))
            self.copies.send(ref, self.passed[k - 1], p.at_head(p.row, 1 - p.core))

    def finish(self):
        p = self.place
        other = p.at_head(p.row, 1 - p.core)
        self.copies.wait(self.buf.at[self.slot(0, 1 - p.core)], self.own[0], other)
        for k in self.order():
            self.copies.wait(self.buf.at[self.slot(k, 1 - p.core)], self.passed[k - 1], other)


def dot(a, b):
    return jnp.dot(a, b, preferred_element_type=F32)


def dot_nt(a, b):
    return lax.dot_general(a, b, (((1,), (1,)), ((), ())), preferred_element_type=F32)


def across(row, size):
    return jnp.transpose(jnp.broadcast_to(row, (size, row.shape[1])))


def vision(patches, gain, weight, bias, windows, count):
    tok = patches.shape[0]
    values = patches.astype(F32)
    normed = values * lax.rsqrt(jnp.mean(values * values, axis=-1, keepdims=True) + EPSILON) * gain
    mixed = (dot(normed.astype(BF16), weight) + bias).astype(BF16)
    width = mixed.shape[1]
    parts = width // VHD
    heads = parts // 3
    row, col = iota((width, parts * 128), 0), iota((width, parts * 128), 1)
    lane = col & 127
    spread = jnp.where((row == (col >> 7) * VHD + lane) & (lane < VHD), 1.0, 0.0).astype(BF16)
    wide = dot(mixed, spread).astype(BF16)
    down = across(windows, tok)
    row, col = iota((tok, tok), 0), iota((tok, tok), 1)
    allowed = (down == windows) & ((col < count) | (row == col))
    results = []
    for h in range(heads):
        query, key, value = (wide[:, (3 * h + i) * 128 : (3 * h + i + 1) * 128] for i in range(3))
        scores = jnp.where(allowed, dot_nt(query, key) * (1.0 / math.sqrt(VHD)), MASKED)
        top = jnp.max(scores, axis=-1, keepdims=True)
        weights = jnp.where(allowed, jnp.exp(scores - top), 0.0)
        total = jnp.sum(weights, axis=-1, keepdims=True)
        results.append((dot(weights.astype(BF16), value) / total).astype(BF16))
    both = jnp.concatenate(results, axis=1)
    row, col = iota((heads * 128, heads * VHD), 0), iota((heads * 128, heads * VHD), 1)
    lane = row & 127
    pack = jnp.where((col == (row >> 7) * VHD + lane) & (lane < VHD), 1.0, 0.0).astype(BF16)
    return dot(both, pack).astype(BF16)


def widen(merged, blocks):
    share = merged.shape[1] // (PAIR * DEEP * WIDE)
    span = blocks * share
    row, col = iota((span, blocks * 32), 0), iota((span, blocks * 32), 1)
    main = col < blocks * 16
    near = jnp.where(main, col, col - blocks * 16)
    block, place = near >> 4, near & 15
    want = block * share + jnp.where(main, place, 16 + (place & 3))
    spread = jnp.where(row == want, 1.0, 0.0).astype(BF16)
    return [
        dot(merged[:, at * span : (at + 1) * span], spread).astype(BF16)
        for at in range(merged.shape[1] // span)
    ]


def turn(x, cosine, sine):
    return x * cosine + pltpu.roll(x, HD // 2, 1) * sine


def attend(state, query, keys, values, allowed):
    scores = dot_nt(query, keys) * (1.0 / math.sqrt(HD))
    if allowed is not None:
        scores = jnp.where(allowed, scores, MASKED)
    here = jnp.max(scores, axis=-1, keepdims=True)
    if state is None:
        top = here
    else:
        top = jnp.maximum(state[0], here)
    weights = jnp.exp(scores - top)
    if allowed is not None:
        weights = jnp.where(allowed, weights, 0.0)
    total = jnp.sum(weights, axis=-1, keepdims=True)
    result = dot(weights.astype(BF16), values)
    if state is not None:
        factor = jnp.exp(state[0] - top)
        total = state[1] * factor + total
        result = state[2] * factor + result
    return top, total, result


def kernel(
    patches,
    count,
    token_patch,
    windows,
    text,
    vit_gain,
    vit_qkv,
    vit_bias,
    vit_proj,
    proj_bias,
    merge_gain,
    merger,
    merger_bias,
    llm_gain,
    w_qkv,
    qkv_bias,
    out,
    merge_buf,
    weight_buf,
    proj_buf,
    att_buf,
    stitch_buf,
    kv_buf,
    query_buf,
    local_sems,
    send_sems,
    recv_sems,
):
    place = Place()
    p = place
    barrier = pltpu.get_barrier_semaphore()
    around = p.neighbours()
    for device in around:
        pl.semaphore_signal(barrier, inc=1, device_id=device, device_id_type=pl.DeviceIdType.MESH)
    local = [
        pltpu.make_async_copy(merger, merge_buf.at[p.pair, p.deep, p.wide], local_sems.at[0]),
        pltpu.make_async_copy(w_qkv, weight_buf.at[p.pair, p.deep, p.wide], local_sems.at[1]),
        pltpu.make_async_copy(vit_proj, proj_buf.at[p.head], local_sems.at[2]),
    ]
    for copy in local:
        copy.start()
    for copy in local:
        copy.wait()
    pl.semaphore_wait(barrier, len(around))

    tok, features = patches.shape
    width = text.shape[1]
    columns = w_qkv.shape[1]
    every = slice(None)
    copies = Copies(send_sems, recv_sems)
    cut = (merger.shape[1] // 256) * 128
    merge_gather = CtxGather(copies, p, merge_buf, (every, slice(0, cut)), (every, slice(cut, None)))
    cut = (columns // 256) * 128
    weight_gather = CtxGather(copies, p, weight_buf, (every, slice(0, cut)), (every, slice(cut, None)))
    cut = tok // 2
    kv_gather = CtxGather(copies, p, kv_buf, (slice(0, cut), every), (slice(cut, None), every))
    proj_gather = HeadGather(copies, p, proj_buf)
    att_gather = HeadGather(copies, p, att_buf)
    stitch_gather = HeadGather(copies, p, stitch_buf)

    merge_gather.start()
    weight_gather.start()
    proj_gather.start()

    att_buf[p.head] = vision(
        patches[...], vit_gain[...], vit_qkv[...], vit_bias[...], windows[...], count[...]
    )
    merge_gather.swapped()
    weight_gather.swapped()
    att_gather.start()
    while not merge_gather.done():
        merge_gather.tick()
        if merge_gather.ticks % 2 == 0 and weight_gather.ticks < 2:
            weight_gather.tick()
    att_gather.pass_on()
    proj_gather.pass_on()
    weight_gather.tick()
    att_gather.finish()
    proj_gather.finish()

    vit_out = patches[...].astype(F32) + proj_bias[...]
    for h in range(ROWS * CORES):
        vit_out += dot(att_buf[h], proj_buf[h])
    merged = vit_out * lax.rsqrt(jnp.mean(vit_out * vit_out, axis=-1, keepdims=True) + EPSILON)
    merged = (merged * merge_gain[...]).astype(BF16)
    blocks = DEEP * WIDE
    spreads = widen(merged, blocks)
    image = jnp.broadcast_to(merger_bias[...], (tok, width))
    tails = [jnp.zeros((tok, 128), F32) for _ in range(4)]
    for g in range(PAIR):
        rows = merge_buf[g].reshape(blocks * 16, merger.shape[1])
        image += dot(spreads[g][:, : blocks * 16], rows[:, :width])
        rest = spreads[g][:, blocks * 16 :]
        lane = iota(rest.shape, 1)
        for j in range(4):
            chosen = jnp.where(((lane >> 2) & 3) == j, rest.astype(F32), 0.0).astype(BF16)
            tails[j] += dot(chosen, rows[:, width:])
    image = (image + jnp.concatenate(tails, axis=1)).astype(BF16)
    down = across(token_patch[...], tok)
    chosen = jnp.where(down == iota((tok, tok), 1), 1.0, 0.0).astype(BF16)
    picked = dot(chosen, image)
    stitch_buf[p.head] = jnp.where(down[:, :1] >= 0, picked, text[...].astype(F32)).astype(BF16)
    stitch_gather.start()

    lane = iota((tok, HD), 1)
    step = (lane & (HD // 2 - 1)).astype(F32) * (2.0 / HD)
    angle = (p.ctx * tok + iota((tok, HD), 0)).astype(F32) * jnp.exp(-math.log(THETA) * step)
    cosine = jnp.cos(angle)
    sine = jnp.where(lane < HD // 2, -1.0, 1.0) * jnp.sin(angle)

    weight_gather.tick()
    stitch_gather.pass_on()
    weight_gather.tick()
    stitch_gather.finish()
    while not weight_gather.done():
        weight_gather.tick()

    square = jnp.zeros((tok, width), F32)
    for h in range(ROWS * CORES):
        block = stitch_buf[h].astype(F32)
        square += block * block
    scale = lax.rsqrt(jnp.sum(square, axis=-1, keepdims=True) / (ROWS * CORES * width) + EPSILON)
    projected = jnp.broadcast_to(qkv_bias[...], (tok, columns))
    span = width // w_qkv.shape[0]
    for h in range(ROWS * CORES):
        block = (stitch_buf[h].astype(F32) * scale * llm_gain[:, h * width : (h + 1) * width]).astype(BF16)
        first = h * span
        if span >= WIDE:
            rows = weight_buf[first // (DEEP * WIDE), pl.ds((first // WIDE) % DEEP, span // WIDE)]
        else:
            rows = weight_buf[first // (DEEP * WIDE), (first // WIDE) % DEEP, pl.ds(first % WIDE, span)]
        projected += dot(block, rows.reshape(width, columns))
    key = turn(projected[:, QH * HD : (QH + 1) * HD], cosine, sine).astype(BF16)
    kv_buf[p.pair, p.deep, p.wide, :, :HD] = key
    kv_buf[p.pair, p.deep, p.wide, :, HD:] = projected[:, (QH + 1) * HD :].astype(BF16)
    for j in range(QH):
        query_buf[j * tok : (j + 1) * tok] = turn(
            projected[:, j * HD : (j + 1) * HD], cosine, sine
        ).astype(BF16)
    kv_gather.start()
    kv_gather.swapped()
    while not kv_gather.done():
        kv_gather.tick()

    query = query_buf[...]
    group = p.pair * DEEP + p.deep
    keys = WIDE * tok
    rows, cols = iota((QH * tok, keys), 0), iota((QH * tok, keys), 1)
    allowed = cols <= p.wide * tok + (rows & (tok - 1))
    own = kv_buf[p.pair, p.deep].reshape(keys, 2 * HD)
    state = attend(None, query, own[:, :HD], own[:, HD:], allowed)

    def visit(unit, state):
        block = kv_buf[unit // DEEP, unit % DEEP].reshape(keys, 2 * HD)
        return attend(state, query, block[:, :HD], block[:, HD:], None)

    _, total, result = lax.fori_loop(0, group, visit, state)
    result = (result / total).astype(BF16)
    for j in range(QH):
        out[:, j * HD : (j + 1) * HD] = result[j * tok : (j + 1) * tok]
    copies.drain()


def body(
    patches,
    patch_count,
    token_patch,
    window_ids,
    text_embed,
    vit_norm_gain,
    vit_qkv,
    vit_qkv_bias,
    vit_proj,
    vit_proj_bias,
    merge_norm_gain,
    merger,
    merger_bias,
    llm_norm_gain,
    w_qkv,
    qkv_bias,
):
    tok, features = patches.shape
    share, width = merger.shape
    rest = merger[16:].reshape(4, width // 128, 128)
    rest = jnp.transpose(rest, (1, 0, 2)).reshape(16, 128)
    merger_tile = jnp.concatenate([merger[:16], rest], axis=1)
    line = lambda vector: vector.reshape(1, -1)
    vmem = pl.BlockSpec(memory_space=pltpu.VMEM)
    hbm = pl.BlockSpec(memory_space=pltpu.HBM)
    specs = [vmem] * 16
    specs[8] = specs[11] = specs[14] = hbm
    ctx_shape = (PAIR, DEEP, WIDE)
    heads = ROWS * CORES
    per_ctx = 1 + 2 * (WIDE - 1 + DEEP - 1) * PAIR
    slots = 3 * per_ctx + 3 * (2 * ROWS - 1)
    return pl.pallas_call(
        kernel,
        out_shape=jax.ShapeDtypeStruct((tok, QH * HD), BF16),
        in_specs=specs,
        out_specs=vmem,
        scratch_shapes=[
            pltpu.VMEM(ctx_shape + merger_tile.shape, BF16),
            pltpu.VMEM(ctx_shape + w_qkv.shape, BF16),
            pltpu.VMEM((heads,) + vit_proj.shape, BF16),
            pltpu.VMEM((heads, tok, vit_proj.shape[0]), BF16),
            pltpu.VMEM((heads,) + text_embed.shape, BF16),
            pltpu.VMEM(ctx_shape + (tok, 2 * HD), BF16),
            pltpu.VMEM((QH * tok, HD), BF16),
            pltpu.SemaphoreType.DMA((3,)),
            pltpu.SemaphoreType.DMA((slots,)),
            pltpu.SemaphoreType.DMA((slots,)),
        ],
        compiler_params=pltpu.CompilerParams(
            collective_id=0, has_side_effects=True, vmem_limit_bytes=60 * 1024 * 1024
        ),
        name="whole",
    )(
        patches,
        patch_count.reshape(1, 1),
        line(token_patch),
        line(window_ids),
        text_embed,
        line(vit_norm_gain),
        vit_qkv,
        line(vit_qkv_bias),
        vit_proj,
        line(vit_proj_bias),
        line(merge_norm_gain),
        merger_tile,
        line(merger_bias),
        line(llm_norm_gain),
        w_qkv,
        line(qkv_bias),
    )


def solution(mesh):
    return jax.shard_map(
        body,
        mesh=mesh,
        in_specs=(
            P("ctx", None),
            P("ctx"),
            P("ctx"),
            P("ctx"),
            P("ctx", "head"),
            P(),
            P(None, "head"),
            P("head"),
            P("head", None),
            P(),
            P(),
            P("ctx", "head"),
            P("head"),
            P(),
            P("ctx", "head"),
            P("head"),
        ),
        out_specs=P("ctx", "head"),
        check_vma=False,
    )
```

time: 1010 us -> 166 us (0.16)
  the two profiles are of different devices: /device:TPU:494 before, /device:TPU:24 now
where the time goes in v1:
time: 166 us; the launch traced here: 165 us
  Pallas kernels  153 us (92%)
  local copies, waits for them, and re-layouts  10.6 us (6%)
    pallas_call x1, Pallas kernels, body(): pl.pallas_call(kernel, out_shape=jax.ShapeDtypeStruct((tok, QH * HD), BF1...  153 us
    reshape x4, local copies, waits for them, and re-layouts, body(): line = lambda vector: vector.reshape(1, -1)  5.14 us
    unnamed x2, local copies, waits for them, and re-layouts  3.99 us

profile of v1, /device:TPU:24, one launch (start us, length us, event | category | flops | bytes accessed | tf_op | source)
XLA Modules:
  0.0 165.2 jit_solution(6848014631995933817)
XLA Ops:
  0.7 1.3 reshape.47.qkv_bias
  1.9 0.7 slice.7
  2.6 1.3 reshape.39.vit_gain
  3.9 1.3 reshape.41.proj_bias
  5.2 1.3 reshape.42.merge_gain
  6.5 0.7 slice.6
  7.2 0.6 pad_maximum_fusion.merger
  7.8 2.4 %copy.18.vit_qkv = bf16[1280,480]{1,0:T(8,128)(2,1)} copy(bf16[1280,480]{0,1:T(8,128)(2,1)} %param.22) | data formatting | bytes 2457600 | tf_op args[6]
  10.3 153.3 %whole.1 = bf16[128,512]{1,0:T(8,128)(2,1)} custom-call(bf16[128,1280]{1,0:T(8,128)(2,1)} %patches.1, s32[1,1]{1,0:T(1,128)} %bitcast.11.count, s32[1,128]{1,0:T(1,128)} %bitcast.16, s32[1,128]{1,0:T(1,128)} %bitcast.17, bf16[128,512]{1,0:T(8,128)(2,1)} %text.1, f32[1,1280]{1,0:T(1,128)} %reshape.39.vit_gain, bf16[1280,480]{1,0:T(8,128)(2,1)} %copy.18.vit_qkv, ...), custom_call_target="tpu_custom_call" | custom-call | tf_op jit(solution)/shard_map/whole/pallas_call | solution.py:507
  163.6 1.6 copy.21

commit v2 on v1

v2 whole, which is shorter than its diff:
```python
import functools
import math

import jax
import jax.numpy as jnp
from jax import lax
from jax.experimental import pallas as pl
from jax.experimental.pallas import tpu as pltpu
from jax.sharding import PartitionSpec as P

VHD = 80
HD = 128
QH = 4
EPSILON = 1e-06
THETA = 1000000.0
MASKED = -1e30

PAIR, DEEP, WIDE = 2, 8, 4
ROWS, CORES = 4, 2
F32 = jnp.float32
BF16 = jnp.bfloat16


def iota(shape, dim):
    return lax.broadcasted_iota(jnp.int32, shape, dim)


class Place:
    def __init__(self):
        ctx = lax.axis_index("ctx")
        head = lax.axis_index("head")
        self.ctx, self.head = ctx, head
        self.pair = ctx // (DEEP * WIDE)
        self.deep = (ctx // WIDE) % DEEP
        self.wide = ctx % WIDE
        self.row = head // CORES
        self.core = head % CORES
        self.high = self.row * PAIR + self.pair
        self.sign = 1 - 2 * self.core
        self.side = 2 * self.pair - 1

    def at_ctx(self, pair, deep, wide):
        return ((pair * DEEP + deep) * WIDE + wide, self.head)

    def at_head(self, row, core):
        return (self.ctx, row * CORES + core)

    def at_high(self, step):
        high = self.high_at(step)
        ctx = ((high % PAIR) * DEEP + self.deep) * WIDE + self.wide
        return (ctx, (high // PAIR) * CORES + self.core)

    def high_at(self, step):
        return (self.high + step + 2 * ROWS * PAIR) % (ROWS * PAIR)

    def other_core(self):
        return self.at_head(self.row, 1 - self.core)

    def other_pair(self):
        return self.at_ctx(1 - self.pair, self.deep, self.wide)

    def next_pair(self):
        return self.at_high(self.side)

    def deep_at(self, step):
        return (self.deep + step + 2 * DEEP) % DEEP

    def wide_at(self, step):
        return (self.wide + step + 2 * WIDE) % WIDE

    def at_deep(self, step):
        return self.at_ctx(self.pair, self.deep_at(step), self.wide)

    def at_wide(self, step):
        return self.at_ctx(self.pair, self.deep, self.wide_at(step))

    def neighbours(self):
        found = [self.other_pair(), self.next_pair(), self.at_deep(1), self.at_deep(-1)]
        found += [self.at_wide(k) for k in range(1, WIDE)]
        found += [self.at_head((self.row + k) % ROWS, self.core) for k in range(1, ROWS)]
        found.append(self.other_core())
        return found


class Copies:
    def __init__(self, send_sems, recv_sems):
        self.send_sems, self.recv_sems = send_sems, recv_sems
        self.used = 0
        self.sent = []

    def take(self, count):
        self.used += count
        return list(range(self.used - count, self.used))

    def copy(self, source, target, slot, device):
        return pltpu.make_async_remote_copy(
            src_ref=source,
            dst_ref=target,
            send_sem=self.send_sems.at[slot],
            recv_sem=self.recv_sems.at[slot],
            device_id=device,
            device_id_type=pl.DeviceIdType.MESH,
        )

    def send(self, make, slot, device, target=None, some=False):
        self.copy(make(), (target or make)(), slot, device()).start()
        self.sent.append((make, target or make, slot, device, some))

    def wait(self, ref, slot, device):
        self.copy(ref, ref, slot, device).wait_recv()

    def drain(self, some):
        for make, target, slot, device, kind in self.sent:
            if kind == some:
                self.copy(make(), target(), slot, device()).wait_send()


class PlaneGather:
    def __init__(self, copies, place, buf, rows, some=(False, False)):
        self.copies, self.place, self.buf, self.some = copies, place, buf, some
        self.first, self.second = slice(0, rows), slice(rows, None)
        self.early = [copies.take(WIDE - 1) for _ in range(2)]
        self.bundles = [copies.take(DEEP) for _ in range(2)]
        self.singles = [copies.take(DEEP) for _ in range(2)]
        self.across = [[copies.take(WIDE - 1) for _ in range(DEEP)] for _ in range(2)]

    def offset(self, t):
        return self.place.sign * ((t + 1) // 2) * (-1 if t % 2 else 1)

    def way(self, t):
        return self.place.sign * (1 if t % 2 else -1)

    def bundle(self, pair, t):
        return self.buf.at[pair, self.place.deep_at(self.offset(t)), :, self.first]

    def single(self, pair, t, step=0):
        p = self.place
        return self.buf.at[pair, p.deep_at(self.offset(t)), p.wide_at(step), self.second]

    def along(self, slots, make, j, t):
        p = self.place
        for later in (1, 2) if t == 0 else (t + 2,):
            if later < DEEP:
                self.copies.send(
                    make, slots[j][later], lambda later=later: p.at_deep(self.way(later)), some=self.some[j]
                )

    def sideways(self, pair, j, t):
        p = self.place
        for k, step in ((0, 1), (1, -1)):
            self.copies.send(
                lambda: self.single(pair, t),
                self.across[j][t][k],
                lambda step=step: p.at_wide(p.sign * step),
                some=self.some[j],
            )

    def start(self, pair, j):
        p = self.place
        self.along(self.singles, lambda: self.single(pair, 0), j, 0)
        for k in range(1, WIDE):
            self.copies.send(
                lambda: self.buf.at[pair, p.deep, p.wide, self.first],
                self.early[j][k - 1],
                lambda k=k: p.at_wide(k),
                some=self.some[j],
            )
        self.sideways(pair, j, 0)

    def arrive(self, pair, j, t):
        p = self.place
        if t == 0:
            for k in range(1, WIDE):
                ref = self.buf.at[pair, p.deep, p.wide_at(-k), self.first]
                self.copies.wait(ref, self.early[j][k - 1], p.other_core())
            self.along(self.bundles, lambda: self.bundle(pair, 0), j, 0)
        else:
            self.copies.wait(self.single(pair, t), self.singles[j][t], p.other_core())
            self.along(self.singles, lambda: self.single(pair, t), j, t)
            self.sideways(pair, j, t)
            self.copies.wait(self.bundle(pair, t), self.bundles[j][t], p.other_core())
            self.along(self.bundles, lambda: self.bundle(pair, t), j, t)

    def pass_on(self, pair, j, t):
        p = self.place
        self.copies.wait(self.single(pair, t, -p.sign), self.across[j][t][0], p.other_core())
        self.copies.send(
            lambda: self.single(pair, t, -p.sign),
            self.across[j][t][2],
            lambda: p.at_wide(p.sign),
            some=self.some[j],
        )

    def finish(self, pair, j, t):
        p = self.place
        self.copies.wait(self.single(pair, t, p.sign), self.across[j][t][1], p.other_core())
        self.copies.wait(self.single(pair, t, -2 * p.sign), self.across[j][t][2], p.other_core())

    def step(self, pair, j, t):
        if t < DEEP:
            self.arrive(pair, j, t)
        if 0 <= t - 1 < DEEP:
            self.pass_on(pair, j, t - 1)
        if 0 <= t - 2 < DEEP:
            self.finish(pair, j, t - 2)


class HeadGather:
    def __init__(self, copies, place, buf):
        self.copies, self.place, self.buf = copies, place, buf
        self.own = copies.take(ROWS)
        self.passed = copies.take(ROWS)

    def block(self, back, core):
        return self.buf.at[((self.place.row - back + ROWS) % ROWS) * CORES + core]

    def start(self):
        p = self.place
        for k in range(1, ROWS):
            self.copies.send(
                lambda: self.buf.at[p.head],
                self.own[k],
                lambda k=k: p.at_head((p.row + k) % ROWS, p.core),
            )
        self.copies.send(lambda: self.buf.at[p.head], self.own[0], p.other_core)

    def pass_on(self):
        p = self.place
        for k in (1, 3, 2):
            self.copies.wait(self.block(k, p.core), self.own[k], p.other_core())
            self.copies.send(lambda k=k: self.block(k, p.core), self.passed[k], p.other_core)

    def finish(self):
        p = self.place
        self.copies.wait(self.block(0, 1 - p.core), self.own[0], p.other_core())
        for k in (1, 3, 2):
            self.copies.wait(self.block(k, 1 - p.core), self.passed[k], p.other_core())


class ProjGather:
    def __init__(self, copies, place, buf):
        self.copies, self.place, self.buf = copies, place, buf
        self.slots = copies.take(6)
        self.passed = copies.take(7)

    def half(self, step, core, half):
        rows = self.buf.shape[1] // 2
        row = (self.place.row + step + ROWS) % ROWS
        return self.buf.at[row * CORES + core, pl.ds(pl.multiple_of(half * rows, 16), rows)]

    def piece(self, event, core):
        p = self.place
        step = (p.side, p.side, -p.side, -p.side, 2, 2)[event]
        half = (p.pair, 1 - p.pair, 1 - p.pair, p.pair, p.pair, 1 - p.pair)[event]
        return self.half(step, core, half)

    def start(self):
        p = self.place
        for event, half in ((0, 1 - p.pair), (1, p.pair)):
            self.copies.send(lambda half=half: self.half(0, p.core, half), self.slots[event], p.next_pair)
        self.copies.send(lambda: self.buf.at[p.head], self.passed[6], p.other_core)

    def event(self, event):
        p = self.place
        make = lambda: self.piece(event, p.core)
        self.copies.wait(make(), self.slots[event], p.other_core())
        if event in (0, 1):
            self.copies.send(make, self.slots[event + 2], p.other_pair)
        if event == 2:
            self.copies.send(make, self.slots[4], p.next_pair)
        if event == 4:
            self.copies.send(make, self.slots[5], p.other_pair)
        self.copies.send(make, self.passed[event], p.other_core)

    def finish(self):
        p = self.place
        other = 1 - p.core
        self.copies.wait(self.buf.at[p.row * CORES + other], self.passed[6], p.other_core())
        for event in range(6):
            self.copies.wait(self.piece(event, other), self.passed[event], p.other_core())


class RingGather:
    def __init__(self, copies, place, buf, pieces):
        self.copies, self.place, self.buf, self.pieces = copies, place, buf, pieces
        self.size = ROWS * PAIR
        self.slots = [copies.take(self.size) for _ in range(pieces)]
        self.passed = [copies.take(self.size) for _ in range(pieces)]

    def piece(self, t, core, i, sign):
        rows = self.buf.shape[2] // self.pieces
        offset = sign * ((t + 1) // 2) * (-1 if t % 2 else 1)
        return self.buf.at[self.place.high_at(offset), core, i * rows : (i + 1) * rows]

    def send(self, t, i):
        p = self.place
        make = lambda: self.piece(t, p.core, i, p.sign)
        for later in (1, 2) if t == 0 else (t + 2,):
            if later < self.size:
                step = p.sign * (1 if later % 2 else -1)
                self.copies.send(make, self.slots[i][later], lambda step=step: p.at_high(step))
        self.copies.send(make, self.passed[i][t], p.other_core)

    def start(self):
        for i in range(self.pieces):
            self.send(0, i)

    def step(self, t):
        p = self.place
        for i in range(self.pieces):
            self.copies.wait(self.piece(t, p.core, i, p.sign), self.slots[i][t], p.other_core())
            self.send(t, i)

    def finish(self):
        p = self.place
        for t in range(self.size):
            for i in range(self.pieces):
                self.copies.wait(self.piece(t, 1 - p.core, i, -p.sign), self.passed[i][t], p.other_core())


def dot(a, b):
    return jnp.dot(a, b, preferred_element_type=F32)


def dot_nt(a, b):
    return lax.dot_general(a, b, (((1,), (1,)), ((), ())), preferred_element_type=F32)


def across(row, size):
    return jnp.transpose(jnp.broadcast_to(row, (size, row.shape[1])))


def vision(patches, gain, weight, bias, windows, count):
    tok = patches.shape[0]
    values = patches.astype(F32)
    normed = values * lax.rsqrt(jnp.mean(values * values, axis=-1, keepdims=True) + EPSILON) * gain
    mixed = (dot_nt(normed.astype(BF16), weight) + bias).astype(BF16)
    width = mixed.shape[1]
    parts = width // VHD
    heads = parts // 3
    row, col = iota((width, parts * 128), 0), iota((width, parts * 128), 1)
    lane = col & 127
    spread = jnp.where((row == (col >> 7) * VHD + lane) & (lane < VHD), 1.0, 0.0).astype(BF16)
    wide = dot(mixed, spread).astype(BF16)
    down = across(windows, tok)
    row, col = iota((tok, tok), 0), iota((tok, tok), 1)
    allowed = (down == windows) & ((col < count) | (row == col))
    results = []
    for h in range(heads):
        query, key, value = (wide[:, (3 * h + i) * 128 : (3 * h + i + 1) * 128] for i in range(3))
        scores = jnp.where(allowed, dot_nt(query, key) * (1.0 / math.sqrt(VHD)), MASKED)
        top = jnp.max(scores, axis=-1, keepdims=True)
        weights = jnp.where(allowed, jnp.exp(scores - top), 0.0)
        total = jnp.sum(weights, axis=-1, keepdims=True)
        results.append((dot(weights.astype(BF16), value) / total).astype(BF16))
    both = jnp.concatenate(results, axis=1)
    row, col = iota((heads * 128, heads * VHD), 0), iota((heads * 128, heads * VHD), 1)
    lane = row & 127
    pack = jnp.where((col == (row >> 7) * VHD + lane) & (lane < VHD), 1.0, 0.0).astype(BF16)
    return dot(both, pack).astype(BF16)


def widen(merged, blocks):
    share = merged.shape[1] // (PAIR * DEEP * WIDE)
    span = blocks * share
    row, col = iota((span, blocks * 32), 0), iota((span, blocks * 32), 1)
    main = col < blocks * 16
    near = jnp.where(main, col, col - blocks * 16)
    block, place = near >> 4, near & 15
    want = block * share + jnp.where(main, place, 16 + (place & 3))
    spread = jnp.where(row == want, 1.0, 0.0).astype(BF16)
    return [
        dot(merged[:, at * span : (at + 1) * span], spread).astype(BF16)
        for at in range(merged.shape[1] // span)
    ]


def turn(x, cosine, sine):
    return x * cosine + pltpu.roll(x, HD // 2, 1) * sine


def attend(top_ref, total_ref, sum_ref, query_ref, block, allowed):
    keys = block.shape[0] * block.shape[1]
    block = block.reshape(keys, 2 * HD)
    scores = dot_nt(query_ref[...], block[:, :HD]) * (1.0 / math.sqrt(HD))
    if allowed is not None:
        scores = jnp.where(allowed, scores, MASKED)
    top = jnp.max(scores, axis=-1, keepdims=True)
    if allowed is None:
        old = top_ref[...]
        top = jnp.maximum(top, old)
        factor = jnp.exp(old - top)
    weights = jnp.exp(scores - top)
    if allowed is not None:
        weights = jnp.where(allowed, weights, 0.0)
    total = jnp.sum(weights, axis=-1, keepdims=True)
    result = dot(weights.astype(BF16), block[:, HD:])
    if allowed is None:
        total = total_ref[...] * factor + total
        result = sum_ref[...] * factor + result
    top_ref[...] = top
    total_ref[...] = total
    sum_ref[...] = result


def kernel(
    patches,
    count,
    token_patch,
    windows,
    text,
    vit_gain,
    vit_qkv,
    vit_bias,
    vit_proj,
    proj_bias,
    merge_gain,
    merger,
    merger_bias,
    llm_gain,
    w_qkv,
    qkv_bias,
    out,
    merge_buf,
    weight_buf,
    proj_buf,
    att_buf,
    stitch_buf,
    mine_buf,
    theirs_buf,
    kv_buf,
    query_buf,
    top_ref,
    total_ref,
    sum_ref,
    local_sems,
    send_sems,
    recv_sems,
):
    p = Place()
    barrier = pltpu.get_barrier_semaphore()
    around = p.neighbours()
    for device in around:
        pl.semaphore_signal(barrier, inc=1, device_id=device, device_id_type=pl.DeviceIdType.MESH)
    tok, features = patches.shape
    width = text.shape[1]
    columns = w_qkv.shape[1] // 2
    line = lambda ref: ref[...].reshape(1, -1)

    def half(pair):
        return w_qkv.at[:, pl.ds(pl.multiple_of(pair * columns, 128), columns)]

    local = [
        pltpu.make_async_copy(half(p.pair), weight_buf.at[p.pair, p.deep, p.wide], local_sems.at[0]),
        pltpu.make_async_copy(vit_proj, proj_buf.at[p.head], local_sems.at[1]),
    ]
    for copy in local:
        copy.start()
    rest = merger[16:].astype(F32)
    rest = jnp.concatenate([rest[:, j * 128 : (j + 1) * 128] for j in range(4)], axis=0)
    merge_buf[p.pair, p.deep, p.wide, :, :width] = merger[:16]
    merge_buf[p.pair, p.deep, p.wide, :, width:] = rest.astype(BF16)
    for copy in local:
        copy.wait()
    pl.semaphore_wait(barrier, len(around))

    copies = Copies(send_sems, recv_sems)
    swaps = copies.take(3)
    merge_gather = PlaneGather(copies, p, merge_buf, 8)
    weight_gather = PlaneGather(copies, p, weight_buf, w_qkv.shape[0] // 2)
    kv_gather = PlaneGather(copies, p, kv_buf, tok // 2, (False, True))
    proj_gather = ProjGather(copies, p, proj_buf)
    att_gather = HeadGather(copies, p, att_buf)
    stitch_gather = RingGather(copies, p, stitch_buf, 2)

    own = lambda buf: buf.at[p.pair, p.deep, p.wide]
    copies.send(lambda: own(merge_buf), swaps[0], p.other_pair)
    copies.send(lambda: half(1 - p.pair), swaps[1], p.other_pair, lambda: own(weight_buf))
    merge_gather.start(p.pair, 0)
    proj_gather.start()
    weight_gather.start(p.pair, 0)

    att_buf[p.head] = vision(
        patches[...], line(vit_gain), vit_qkv[...], line(vit_bias), line(windows), count[...]
    )
    for gather, buf, slot in ((merge_gather, merge_buf, 0), (weight_gather, weight_buf, 1)):
        copies.wait(buf.at[1 - p.pair, p.deep, p.wide], swaps[slot], p.other_pair())
        gather.start(1 - p.pair, 1)
    att_gather.start()

    def both(t):
        for gather in (merge_gather, weight_gather):
            gather.step(p.pair, 0, t)
            gather.step(1 - p.pair, 1, t)

    both(0)
    both(1)
    proj_gather.event(0)
    both(2)
    proj_gather.event(1)
    both(3)
    proj_gather.event(2)
    att_gather.pass_on()
    both(4)
    proj_gather.event(3)
    both(5)
    proj_gather.event(4)
    both(6)
    proj_gather.event(5)
    for t in range(7, DEEP + 2):
        merge_gather.step(p.pair, 0, t)
        merge_gather.step(1 - p.pair, 1, t)
    att_gather.finish()
    proj_gather.finish()

    vit_out = patches[...].astype(F32) + line(proj_bias)
    for h in range(ROWS * CORES):
        vit_out += dot(att_buf[h], proj_buf[h])
    merged = vit_out * lax.rsqrt(jnp.mean(vit_out * vit_out, axis=-1, keepdims=True) + EPSILON)
    merged = (merged * line(merge_gain)).astype(BF16)
    blocks = DEEP * WIDE
    spreads = widen(merged, blocks)
    image = jnp.broadcast_to(line(merger_bias), (tok, width))
    tails = [jnp.zeros((tok, 128), F32) for _ in range(4)]
    for g in range(PAIR):
        rows = merge_buf[g].reshape(blocks * 16, width + 128)
        image += dot(spreads[g][:, : blocks * 16], rows[:, :width])
        rest = spreads[g][:, blocks * 16 :]
        lane = iota(rest.shape, 1)
        for j in range(4):
            chosen = jnp.where(((lane >> 2) & 3) == j, rest.astype(F32), 0.0).astype(BF16)
            tails[j] += dot(chosen, rows[:, width:])
    image = (image + jnp.concatenate(tails, axis=1)).astype(BF16)
    down = across(line(token_patch), tok)
    chosen = jnp.where(down == iota((tok, tok), 1), 1.0, 0.0).astype(BF16)
    picked = dot(chosen, image)
    stitch_buf[p.high, p.core] = jnp.where(down[:, :1] >= 0, picked, text[...].astype(F32)).astype(BF16)
    stitch_gather.start()

    lane = iota((PAIR * tok, HD), 1)
    row = iota((PAIR * tok, HD), 0)
    step = (lane & (HD // 2 - 1)).astype(F32) * (2.0 / HD)
    first = (p.deep * WIDE + p.wide) * tok
    position = first + (row & (tok - 1)) + jnp.where(row >= tok, DEEP * WIDE * tok, 0)
    angle = position.astype(F32) * jnp.exp(-math.log(THETA) * step)
    cosine = jnp.cos(angle)
    sine = jnp.where(lane < HD // 2, -1.0, 1.0) * jnp.sin(angle)

    rest = list(range(7, DEEP + 2))
    for t in range(1, ROWS * PAIR):
        if rest and t % 2:
            at = rest.pop(0)
            weight_gather.step(p.pair, 0, at)
            weight_gather.step(1 - p.pair, 1, at)
        stitch_gather.step(t)
    for at in rest:
        weight_gather.step(p.pair, 0, at)
        weight_gather.step(1 - p.pair, 1, at)
    stitch_gather.finish()

    heads = ROWS * CORES
    scales = []
    for q in range(PAIR):
        square = jnp.zeros((tok, width), F32)
        for h in range(heads):
            block = stitch_buf[(h // CORES) * PAIR + q, h % CORES].astype(F32)
            square += block * block
        scales.append(lax.rsqrt(jnp.sum(square, axis=-1, keepdims=True) / (heads * width) + EPSILON))
    bias = qkv_bias[pl.ds(pl.multiple_of(p.pair * columns, 128), columns)].reshape(1, -1)
    projected = jnp.broadcast_to(bias, (PAIR * tok, columns))
    gains = line(llm_gain)
    span = width // w_qkv.shape[0] // WIDE
    for h in range(heads):
        gain = gains[:, h * width : (h + 1) * width]
        block = jnp.concatenate(
            [
                (stitch_buf[(h // CORES) * PAIR + q, h % CORES].astype(F32) * scales[q] * gain).astype(BF16)
                for q in range(PAIR)
            ],
            axis=0,
        )
        first = h * span
        rows = weight_buf[first // DEEP, first % DEEP : first % DEEP + span]
        projected += dot(block, rows.reshape(width, columns))
    for i in (2, 1, 0):
        value = projected[:, i * HD : (i + 1) * HD]
        plain = 3 * p.pair + i == QH + 1
        done = turn(value, jnp.where(plain, 1.0, cosine), jnp.where(plain, 0.0, sine)).astype(BF16)
        for q in range(PAIR):
            mine_buf[q, i] = done[q * tok : (q + 1) * tok]
    copies.send(
        lambda: mine_buf.at[1 - p.pair], swaps[2], p.other_pair, lambda: theirs_buf.at[...]
    )

    @pl.when(p.pair == 1)
    def _():
        for q in range(PAIR):
            kv_buf[q, p.deep, p.wide, :, :HD] = mine_buf[q, 1]
            kv_buf[q, p.deep, p.wide, :, HD:] = mine_buf[q, 2]
        for j in range(QH - 1, QH):
            query_buf[j * tok : (j + 1) * tok] = mine_buf[1, 0]
        kv_gather.start(1, 1)

    copies.wait(theirs_buf.at[...], swaps[2], p.other_pair())

    @pl.when(p.pair == 1)
    def _():
        for j in range(QH - 1):
            query_buf[j * tok : (j + 1) * tok] = theirs_buf[j]

    @pl.when(p.pair == 0)
    def _():
        kv_buf[0, p.deep, p.wide, :, :HD] = theirs_buf[1]
        kv_buf[0, p.deep, p.wide, :, HD:] = theirs_buf[2]
        for j in range(QH - 1):
            query_buf[j * tok : (j + 1) * tok] = mine_buf[0, j]
        query_buf[(QH - 1) * tok :] = theirs_buf[0]

    kv_gather.start(0, 0)
    group = p.pair * DEEP + p.deep
    state = (top_ref, total_ref, sum_ref, query_buf)
    for t in range(DEEP + 2):

        @pl.when(p.pair == 1)
        def _():
            kv_gather.step(1, 1, t)

        kv_gather.step(0, 0, t)
        if t == 2:
            shape = (QH * tok, WIDE * tok)
            rows, cols = iota(shape, 0), iota(shape, 1)
            allowed = cols <= p.wide * tok + (rows & (tok - 1))
            attend(*state, kv_buf[p.pair, p.deep], allowed)
        if t >= 2:
            deep = p.deep_at(kv_gather.offset(t - 2))

            def visit(pair, _):
                @pl.when(pair * DEEP + deep < group)
                def _():
                    attend(*state, kv_buf[pair, deep], None)

                return 0

            lax.fori_loop(0, 1 if t == 2 else PAIR, visit, 0)
    result = (sum_ref[...] / total_ref[...]).astype(BF16)
    for j in range(QH):
        out[:, j * HD : (j + 1) * HD] = result[j * tok : (j + 1) * tok]
    copies.drain(False)

    @pl.when(p.pair == 1)
    def _():
        copies.drain(True)


def body(
    patches,
    patch_count,
    token_patch,
    window_ids,
    text_embed,
    vit_norm_gain,
    vit_qkv,
    vit_qkv_bias,
    vit_proj,
    vit_proj_bias,
    merge_norm_gain,
    merger,
    merger_bias,
    llm_norm_gain,
    w_qkv,
    qkv_bias,
):
    tok = patches.shape[0]
    width = text_embed.shape[1]
    vmem = pl.BlockSpec(memory_space=pltpu.VMEM)
    hbm = pl.BlockSpec(memory_space=pltpu.HBM)
    specs = [vmem] * 16
    specs[8] = specs[14] = hbm
    ctx_shape = (PAIR, DEEP, WIDE)
    heads = ROWS * CORES
    plane = 2 * (WIDE - 1 + 2 * DEEP + DEEP * (WIDE - 1))
    slots = 3 + 3 * plane + 2 * ROWS + 13 + 4 * ROWS * PAIR
    parts = (3, tok, HD)
    return pl.pallas_call(
        kernel,
        out_shape=jax.ShapeDtypeStruct((tok, QH * HD), BF16),
        in_specs=specs,
        out_specs=vmem,
        scratch_shapes=[
            pltpu.VMEM(ctx_shape + (16, width + 128), BF16),
            pltpu.VMEM(ctx_shape + (w_qkv.shape[0], w_qkv.shape[1] // 2), BF16),
            pltpu.VMEM((heads,) + vit_proj.shape, BF16),
            pltpu.VMEM((heads, tok, vit_proj.shape[0]), BF16),
            pltpu.VMEM((ROWS * PAIR, CORES) + text_embed.shape, BF16),
            pltpu.VMEM((PAIR,) + parts, BF16),
            pltpu.VMEM(parts, BF16),
            pltpu.VMEM(ctx_shape + (tok, 2 * HD), BF16),
            pltpu.VMEM((QH * tok, HD), BF16),
            pltpu.VMEM((QH * tok, 1), F32),
            pltpu.VMEM((QH * tok, 1), F32),
            pltpu.VMEM((QH * tok, HD), F32),
            pltpu.SemaphoreType.DMA((2,)),
            pltpu.SemaphoreType.DMA((slots,)),
            pltpu.SemaphoreType.DMA((slots,)),
        ],
        compiler_params=pltpu.CompilerParams(
            collective_id=0, has_side_effects=True, vmem_limit_bytes=60 * 1024 * 1024
        ),
        name="whole",
    )(
        patches,
        patch_count.reshape(1, 1),
        token_patch,
        window_ids,
        text_embed,
        vit_norm_gain,
        vit_qkv.T,
        vit_qkv_bias,
        vit_proj,
        vit_proj_bias,
        merge_norm_gain,
        merger,
        merger_bias,
        llm_norm_gain,
        w_qkv,
        qkv_bias,
    )


def solution(mesh):
    return jax.shard_map(
        body,
        mesh=mesh,
        in_specs=(
            P("ctx", None),
            P("ctx"),
            P("ctx"),
            P("ctx"),
            P("ctx", "head"),
            P(),
            P(None, "head"),
            P("head"),
            P("head", None),
            P(),
            P(),
            P("ctx", "head"),
            P("head"),
            P(),
            P("ctx", "head"),
            P("head"),
        ),
        out_specs=P("ctx", "head"),
        check_vma=False,
    )
```

time: 166 us -> 123 us (0.74)
  the two profiles are of different devices: /device:TPU:24 before, /device:TPU:8 now
where the time goes in v2:
time: 123 us; the launch traced here: 122 us
  Pallas kernels  120 us (98%)
  local copies, waits for them, and re-layouts  1.57 us (1%)
    pallas_call x1, Pallas kernels, body(): pl.pallas_call(kernel, out_shape=jax.ShapeDtypeStruct((tok, QH * HD), BF1...  120 us

profile of v2, /device:TPU:8, one launch (start us, length us, event | category | flops | bytes accessed | tf_op | source)
XLA Modules:
  0.0 122.5 jit_solution(12396672008789710517)
XLA Ops:
  0.7 120.2 %whole.1 = bf16[128,512]{1,0:T(8,128)(2,1)} custom-call(bf16[128,1280]{1,0:T(8,128)(2,1)} %patches.1, s32[1,1]{1,0:T(1,128)} %bitcast.2.count, s32[128]{0:T(128)} %token_patch.1, s32[128]{0:T(128)} %windows.1, bf16[128,512]{1,0:T(8,128)(2,1)} %text.1, f32[1280]{0:T(1024)} %vit_gain.1, bf16[480,1280]{1,0:T(8,128)(2,1)} %bitcast.3, f32[480]{0:T(512)} %vit_bias.1, ...), custom_call_target="tpu_custom_call" | custom-call | tf_op jit(solution)/shard_map/whole/pallas_call | solution.py:684
  120.9 1.6 %copy.19 = bf16[128,512]{1,0:T(8,128)(2,1)} copy(bf16[128,512]{1,0:T(8,128)(2,1)} %whole.1) | data formatting | bytes 262144
